TPU v7x, 128 devices: a whole 4x4x4 slice. The times are simulated.
128 devices in a mesh: expert: 4 (over x_lo, core), shard: 32 (over z, y, x_hi).
Axes of the slice: x: 4 (x_hi: 2, x_lo: 2; x = x_hi * 2 + x_lo), y: 4, z: 4, core: 2. Of those that a mesh axis runs over, the one named last changes fastest.
Arguments:
- master_gate: float32 [64, 2048, 1024], P('expert', 'shard'), may hold values from -0.25 to 0.25
- master_up: float32 [64, 2048, 1024], P('expert', 'shard'), may hold values from -0.25 to 0.25
- master_down: float32 [64, 1024, 2048], P('expert', None, 'shard'), may hold values from -0.375 to 0.375
- router_weight: float32 [2048, 64], P('shard', 'expert'), may hold values from -0.125 to 0.125
- router_gain: float32 [2048], P('shard'), may hold values from 0.25 to 1.75
Outputs:
- final_gate: bfloat16 [64, 2048, 1024], P('expert', None, 'shard')
- final_up: bfloat16 [64, 2048, 1024], P('expert', None, 'shard')
- final_down: bfloat16 [64, 1024, 2048], P('expert', 'shard')
- scale_gate: float32 [64, 1024], P('expert', 'shard')
- scale_up: float32 [64, 1024], P('expert', 'shard')
- scale_down: float32 [64, 1024], P('expert', 'shard')
- serve_router: bfloat16 [2048, 64], replicated
All inputs are finite; a program needn't handle non-finite values.
Results may differ from a plain program's by a relative error of at most 0.001.
Values may be sent and summed in bfloat16 or wider, within the bound.
A program may use at most 128 MiB of HBM per device.

v0:
```python
import jax
import jax.numpy as jnp
from jax import lax
from jax.sharding import Mesh
from jax.sharding import PartitionSpec as P

SHARD = ("shard_0", "shard_1", "shard_2")
EXPERT = ("expert_0", "expert_1")


def total_of_pieces(value, axis):
    return lax.all_gather(value, axis).sum(0)


def in_order(pieces, dim):
    pieces = jnp.moveaxis(pieces, 0, dim)
    lengths = pieces.shape
    return pieces.reshape(*lengths[:dim], lengths[dim] * lengths[dim + 1], *lengths[dim + 2 :])


def gather_in_order(value, axes, order):
    pieces = value[None]
    for k in order:
        pieces = lax.all_gather(pieces, axes[k], axis=0, tiled=True)
    current = [lax.axis_size(axes[k]) for k in reversed(order)]
    pieces = pieces.reshape(*current, *value.shape)
    turned = sorted(range(len(order)), key=lambda place: order[len(order) - 1 - place])
    return pieces.transpose(*turned, *range(len(order), pieces.ndim)).reshape(-1, *value.shape)


def whole_of(value, axes, order, dim):
    return in_order(gather_in_order(value, axes, order), dim)


def on_device(master_gate, master_up, master_down, router_weight, router_gain):
    total_gate, total_up, total_down = (
        total_of_pieces(jnp.sum(master_gate * master_gate, axis=1), SHARD),
        total_of_pieces(jnp.sum(master_up * master_up, axis=1), SHARD),
        total_of_pieces(jnp.sum(master_down * master_down, axis=2), SHARD),
    )
    scale_gate = jnp.sqrt(total_gate)
    scale_up = jnp.sqrt(total_up)
    scale_down = jnp.sqrt(total_down)
    narrow_gate, narrow_up, narrow_down = (
        (master_gate / jnp.expand_dims(scale_gate, 1)).astype(jnp.bfloat16),
        (master_up / jnp.expand_dims(scale_up, 1)).astype(jnp.bfloat16),
        (master_down / jnp.expand_dims(scale_down, 2)).astype(jnp.bfloat16),
    )
    final_gate, final_up = (
        lax.all_to_all(narrow_gate, SHARD, split_axis=2, concat_axis=1, tiled=True),
        lax.all_to_all(narrow_up, SHARD, split_axis=2, concat_axis=1, tiled=True),
    )
    final_down = lax.all_to_all(narrow_down, SHARD, split_axis=1, concat_axis=2, tiled=True)
    scale_gate = lax.dynamic_slice_in_dim(
        scale_gate, lax.axis_index(SHARD) * final_gate.shape[2], final_gate.shape[2], axis=1
    )
    scale_up = lax.dynamic_slice_in_dim(
        scale_up, lax.axis_index(SHARD) * final_up.shape[2], final_up.shape[2], axis=1
    )
    scale_down = lax.dynamic_slice_in_dim(
        scale_down, lax.axis_index(SHARD) * final_down.shape[1], final_down.shape[1], axis=1
    )
    part_router = (router_weight * router_gain[:, None]).astype(jnp.bfloat16)
    row_router = whole_of(part_router, SHARD, (2, 0, 1), 0)
    serve_router = whole_of(row_router, EXPERT, (0, 1), 1)
    return (final_gate, final_up, final_down, scale_gate, scale_up, scale_down, serve_router)


def solution(mesh):
    torus = Mesh(
        mesh.devices.reshape(2, 2, 4, 4, 2),
        ("expert_0", "expert_1", "shard_0", "shard_1", "shard_2"),
    )
    return jax.shard_map(
        on_device,
        mesh=torus,
        in_specs=(
            P(EXPERT, SHARD, None),
            P(EXPERT, SHARD, None),
            P(EXPERT, None, SHARD),
            P(SHARD, EXPERT),
            P(SHARD),
        ),
        out_specs=(
            P(EXPERT, None, SHARD),
            P(EXPERT, None, SHARD),
            P(EXPERT, SHARD, None),
            P(EXPERT, SHARD),
            P(EXPERT, SHARD),
            P(EXPERT, SHARD),
            P(),
        ),
        check_vma=False,
    )
```

profile of v0, /device:TPU:1, one launch (start us, length us, event | category | flops | bytes accessed | tf_op | source)
XLA Modules:
  0.0 398.6 jit_solution(14546526943388077372)
XLA Ops:
  7.2 3.4 multiply_reduce_fusion.2
  10.7 3.4 multiply_reduce_fusion.1
  14.2 3.4 multiply_reduce_fusion
  17.6 8.1 %copy.42 = f32[16,64,1024]{1,0,2:T(8,128)} copy(f32[16,64,1024]{2,1,0:T(8,128)} %param.5) | data formatting | bytes 8388608 | tf_op args[0]
  25.8 57.4 %all-gather.9.cloned.1.call-done = f32[512,1024]{1,0:T(8,128)} async-done(((f32[16,1024]{1,0:T(8,128)}), f32[512,1024]{1,0:T(8,128)}) %all-gather.9.cloned.1.call-update) | async-done | bytes 2097168 | tf_op jit(solution)/shard_map/all_gather | solution.py:12
  85.1 6.9 %fusion.1 = bf16[1024,16,64]{2,1,0:T(8,128)(2,1)} fusion(f32[16,64,1024]{1,0,2:T(8,128)} %copy.42, f32[16,1024]{0,1:T(8,128)S(1)} %copy.41), kind=kLoop, calls=%fused_computation.12 | loop fusion | flops 2097152 | bytes 6356992
  91.9 7.9 %reshape.47 = bf16[32,2,16384]{2,1,0:T(2,128)(2,1)} reshape(bf16[1024,16,64]{2,1,0:T(8,128)(2,1)} %fusion.1) | data formatting | bytes 4194304
  99.8 5.9 %all-to-all-start = ((bf16[32,2,16384]{2,1,0:T(2,128)(2,1)}), bf16[32,2,16384]{2,1,0:T(2,128)(2,1)S(1)}, u32[]{:S(2)}, u32[]{:S(2)}) async-start(bf16[32,2,16384]{2,1,0:T(2,128)(2,1)} %reshape.47), calls=%async_computation | async-start | bytes 4194304 | tf_op jit(solution)/shard_map/all_to_all | solution.py:50
  105.7 8.1 %copy.46 = f32[16,64,1024]{1,0,2:T(8,128)} copy(f32[16,64,1024]{2,1,0:T(8,128)} %param.6) | data formatting | bytes 8388608 | tf_op args[1]
  113.8 51.8 %all-gather.11.cloned.1.call-done = f32[512,1024]{1,0:T(8,128)} async-done(((f32[16,1024]{1,0:T(8,128)}), f32[512,1024]{1,0:T(8,128)}) %all-gather.11.cloned.1.call-update) | async-done | bytes 2097168 | tf_op jit(solution)/shard_map/all_gather | solution.py:12
  167.5 6.9 %fusion.2 = bf16[1024,16,64]{2,1,0:T(8,128)(2,1)} fusion(f32[16,64,1024]{1,0,2:T(8,128)} %copy.46, f32[16,1024]{0,1:T(8,128)S(1)} %copy.45), kind=kLoop, calls=%fused_computation.13 | loop fusion | flops 2097152 | bytes 6356992
  174.4 7.9 %reshape.49 = bf16[32,2,16384]{2,1,0:T(2,128)(2,1)} reshape(bf16[1024,16,64]{2,1,0:T(8,128)(2,1)} %fusion.2) | data formatting | bytes 4194304
  182.2 6.0 %all-to-all-start.1 = ((bf16[32,2,16384]{2,1,0:T(2,128)(2,1)}), bf16[32,2,16384]{2,1,0:T(2,128)(2,1)}, u32[]{:S(2)}, u32[]{:S(2)}) async-start(bf16[32,2,16384]{2,1,0:T(2,128)(2,1)} %reshape.49), calls=%async_computation.1 | async-start | bytes 4194304 | tf_op jit(solution)/shard_map/all_to_all | solution.py:51
  188.3 8.1 %copy.50 = f32[16,1024,64]{2,0,1:T(8,128)} copy(f32[16,1024,64]{1,2,0:T(8,128)} %param.7) | data formatting | bytes 8388608 | tf_op args[2]
  196.4 51.6 %all-gather.13.cloned.1.call-done = f32[512,1024]{1,0:T(8,128)} async-done(((f32[16,1024]{1,0:T(8,128)}), f32[512,1024]{1,0:T(8,128)}) %all-gather.13.cloned.1.call-update) | async-done | bytes 2097168 | tf_op jit(solution)/shard_map/all_gather | solution.py:12
  250.0 6.9 %fusion.3 = bf16[1024,16,64]{2,1,0:T(8,128)(2,1)} fusion(f32[16,1024,64]{2,0,1:T(8,128)} %copy.50, f32[16,1024]{0,1:T(8,128)S(1)} %copy.49), kind=kLoop, calls=%fused_computation.14 | loop fusion | flops 2097152 | bytes 6356992
  256.8 7.9 %reshape.51 = bf16[32,2,16384]{2,1,0:T(2,128)(2,1)} reshape(bf16[1024,16,64]{2,1,0:T(8,128)(2,1)} %fusion.3) | data formatting | bytes 4194304
  264.7 6.0 %all-to-all-start.2 = ((bf16[32,2,16384]{2,1,0:T(2,128)(2,1)}), bf16[32,2,16384]{2,1,0:T(2,128)(2,1)}, u32[]{:S(2)}, u32[]{:S(2)}) async-start(bf16[32,2,16384]{2,1,0:T(2,128)(2,1)} %reshape.51), calls=%async_computation.2 | async-start | bytes 4194304 | tf_op jit(solution)/shard_map/all_to_all | solution.py:53
  270.8 23.2 %all-gather.4 = bf16[2,64,16]{1,2,0:T(8,128)(2,1)S(1)} all-gather(bf16[1,64,16]{1,2,0:T(8,128)(2,1)S(1)} %fusion), channel_id=5, replica_groups=mesh['expert_0'=2,'expert_1'=2,'shard_0'=4,'shard_1'=4,'shard_2'=2] {'sh..., dimensions={0}, use_global_device_ids=true | all-gather | bytes 6144 | tf_op jit(solution)/shard_map/all_gather | solution.py:24
  294.0 10.0 %all_gather.40 = bf16[8,64,16]{1,2,0:T(8,128)(2,1)S(1)} all-gather(bf16[2,64,16]{1,2,0:T(8,128)(2,1)S(1)} %all-gather.4), channel_id=1, replica_groups=mesh['expert_0'=2,'expert_1'=2,'shard_0'=4,'shard_1'=4,'shard_2'=2] {'sh..., dimensions={0}, use_global_device_ids=true | all-gather | bytes 20480 | tf_op jit(solution)/shard_map/all_gather | solution.py:24
  304.0 9.3 %all_gather.41 = bf16[32,64,16]{1,2,0:T(8,128)(2,1)S(1)} all-gather(bf16[8,64,16]{1,2,0:T(8,128)(2,1)S(1)} %all_gather.40), channel_id=1, replica_groups=mesh['expert_0'=2,'expert_1'=2,'shard_0'=4,'shard_1'=4,'shard_2'=2] {'sh..., dimensions={0}, use_global_device_ids=true | all-gather | bytes 81920 | tf_op jit(solution)/shard_map/all_gather | solution.py:24
  313.6 3.8 all_gather.42
  317.4 11.9 %all_gather.43 = bf16[4,2048,16]{1,2,0:T(8,128)(2,1)S(1)} all-gather(bf16[2,2048,16]{1,2,0:T(8,128)(2,1)S(1)} %all_gather.42), channel_id=1, replica_groups=mesh['expert_0'=2,'expert_1'=2,'shard_0'=4,'shard_1'=4,'shard_2'=2] {'ex..., dimensions={0}, use_global_device_ids=true | all-gather | bytes 393216 | tf_op jit(solution)/shard_map/all_gather | solution.py:24
  331.4 4.0 %reshape.48 = bf16[1024,16,64]{2,1,0:T(8,128)(2,1)} reshape(bf16[32,2,16384]{2,1,0:T(2,128)(2,1)S(1)} %all-to-all-done) | data formatting | bytes 4194304
  335.4 6.9 %copy.44 = bf16[16,32,64,32]{2,1,3,0:T(8,128)(2,1)} copy(bf16[16,32,64,32]{2,0,3,1:T(8,128)(2,1)} %bitcast.47) | data formatting | bytes 4194304 | tf_op jit(solution)/shard_map/all_to_all | solution.py:50
  342.2 6.7 %all_to_all.42 = bf16[16,2048,32]{1,2,0:T(8,128)(2,1)} reshape(bf16[16,32,64,32]{2,1,3,0:T(8,128)(2,1)} %copy.44) | data formatting | bytes 4194304 | tf_op jit(solution)/shard_map/all_to_all | solution.py:50
  349.0 7.9 %reshape.50 = bf16[1024,16,64]{2,1,0:T(8,128)(2,1)} reshape(bf16[32,2,16384]{2,1,0:T(2,128)(2,1)} %all-to-all-done.1) | data formatting | bytes 4194304
  356.9 6.9 %copy.48 = bf16[16,32,64,32]{2,1,3,0:T(8,128)(2,1)} copy(bf16[16,32,64,32]{2,0,3,1:T(8,128)(2,1)} %bitcast.48) | data formatting | bytes 4194304 | tf_op jit(solution)/shard_map/all_to_all | solution.py:51
  363.8 6.7 %all_to_all.46 = bf16[16,2048,32]{1,2,0:T(8,128)(2,1)} reshape(bf16[16,32,64,32]{2,1,3,0:T(8,128)(2,1)} %copy.48) | data formatting | bytes 4194304 | tf_op jit(solution)/shard_map/all_to_all | solution.py:51
  370.5 7.9 %reshape.52 = bf16[1024,16,64]{2,1,0:T(8,128)(2,1)} reshape(bf16[32,2,16384]{2,1,0:T(2,128)(2,1)} %all-to-all-done.2) | data formatting | bytes 4194304
  378.5 6.9 %copy.52 = bf16[16,32,32,64]{3,2,1,0:T(8,128)(2,1)} copy(bf16[16,32,32,64]{3,0,1,2:T(8,128)(2,1)} %bitcast.49) | data formatting | bytes 4194304 | tf_op jit(solution)/shard_map/all_to_all | solution.py:53
  385.3 6.7 %all_to_all.50 = bf16[16,32,2048]{2,1,0:T(8,128)(2,1)} reshape(bf16[16,32,32,64]{3,2,1,0:T(8,128)(2,1)} %copy.52) | data formatting | bytes 4194304 | tf_op jit(solution)/shard_map/all_to_all | solution.py:53
  (28 shorter events, 8.3 us)
Async XLA Ops:
  7.2 76.0 %all-gather.9.cloned.1.call-start = ((), (), s32[]{:S(2)}) async-start(), calls=%async_computation.3 | async-start | bytes 2162688 | tf_op jit(solution)/shard_map/all_gather | solution.py:12
  10.7 154.9 %all-gather.11.cloned.1.call-start = ((), (), s32[]{:S(2)}) async-start(), calls=%async_computation.4 | async-start | bytes 2162688 | tf_op jit(solution)/shard_map/all_gather | solution.py:12
  14.1 233.9 %all-gather.13.cloned.1.call-start = ((), (), s32[]{:S(2)}) async-start(), calls=%async_computation.5 | async-start | bytes 2162688 | tf_op jit(solution)/shard_map/all_gather | solution.py:12
  99.8 82.4 %all-to-all-start = ((bf16[32,2,16384]{2,1,0:T(2,128)(2,1)}), bf16[32,2,16384]{2,1,0:T(2,128)(2,1)S(1)}, u32[]{:S(2)}, u32[]{:S(2)}) async-start(bf16[32,2,16384]{2,1,0:T(2,128)(2,1)} %reshape.47), calls=%async_computation | async-start | bytes 4194304 | tf_op jit(solution)/shard_map/all_to_all | solution.py:50
  182.2 82.5 %all-to-all-start.1 = ((bf16[32,2,16384]{2,1,0:T(2,128)(2,1)}), bf16[32,2,16384]{2,1,0:T(2,128)(2,1)}, u32[]{:S(2)}, u32[]{:S(2)}) async-start(bf16[32,2,16384]{2,1,0:T(2,128)(2,1)} %reshape.49), calls=%async_computation.1 | async-start | bytes 4194304 | tf_op jit(solution)/shard_map/all_to_all | solution.py:51
  256.8 14.0 %copy-start = (f32[64,16]{0,1:T(8,128)S(1)}, f32[64,16]{0,1:T(8,128)}, u32[]{:S(2)}) copy-start(f32[64,16]{0,1:T(8,128)} %param.8) | copy-start | bytes 12292
  256.8 14.0 %copy-start.1 = (f32[64]{0:T(128)S(1)}, f32[64]{0:T(128)}, u32[]{:S(2)}) copy-start(f32[64]{0:T(128)} %param.9) | copy-start | bytes 772
  264.7 105.8 %all-to-all-start.2 = ((bf16[32,2,16384]{2,1,0:T(2,128)(2,1)}), bf16[32,2,16384]{2,1,0:T(2,128)(2,1)}, u32[]{:S(2)}, u32[]{:S(2)}) async-start(bf16[32,2,16384]{2,1,0:T(2,128)(2,1)} %reshape.51), calls=%async_computation.2 | async-start | bytes 4194304 | tf_op jit(solution)/shard_map/all_to_all | solution.py:53
Sparse Core Ops, SparseCore 0:
  11.6 71.4 all-gather.8
  86.8 78.7 all-gather.10
  169.2 78.7 all-gather.12
where the time goes:
time: 401 us; the launch traced here: 399 us
  waiting for transfers between devices  161 us (40%)
  local copies, waits for them, and re-layouts  112 us (28%)
  blocking collectives  58.2 us (15%)
  other arithmetic  36 us (9%)
  starting transfers between devices  18.1 us (5%)
  between operations  13.9 us (3%)
    all_gather x3, waiting for transfers between devices, total_of_pieces(): return lax.all_gather(value, axis).sum(0)  161 us
    unnamed x13, local copies, waits for them, and re-layouts  67.8 us
    all_gather x5, blocking collectives, gather_in_order(): pieces = lax.all_gather(pieces, axes[k], axis=0, tiled=True)  58.2 us
    unnamed x4, other arithmetic  20.6 us
    all_to_all x2, local copies, waits for them, and re-layouts, on_device(): lax.all_to_all(narrow_down, SHARD, split_axis=1, concat_axis=2, tiled=True)  13.6 us
    all_to_all x2, local copies, waits for them, and re-layouts, on_device(): lax.all_to_all(narrow_gate, SHARD, split_axis=2, concat_axis=1, tiled=True)  13.6 us
    all_to_all x2, local copies, waits for them, and re-layouts, on_device(): lax.all_to_all(narrow_up, SHARD, split_axis=2, concat_axis=1, tiled=True)  13.6 us
  transfers between devices with their start and end apart: 6, of which 3 were waited for; matrix products, arithmetic and copies ran while one was open for 27% of the time, Pallas kernels for 0%

commit v1 on v0

--- a/solution.py
+++ b/solution.py
@@ -21,7 +21,10 @@
 def gather_in_order(value, axes, order):
     pieces = value[None]
     for k in order:
-        pieces = lax.all_gather(pieces, axes[k], axis=0, tiled=True)
+        devices = lax.axis_size(axes[k])
+        tiles = jnp.stack([pieces for _ in range(devices)])
+        tiles = lax.all_to_all(tiles, axes[k], split_axis=0, concat_axis=0)
+        pieces = jnp.concatenate(tiles, axis=0)
     current = [lax.axis_size(axes[k]) for k in reversed(order)]
     pieces = pieces.reshape(*current, *value.shape)
     turned = sorted(range(len(order)), key=lambda place: order[len(order) - 1 - place])

time: 401 us -> 346 us (0.86)
  waiting for transfers between devices: 161 us -> 121 us
  blocking collectives: 58.2 us -> 26.3 us
  starting transfers between devices: 18.1 us -> 30.1 us
    all_gather x5 -> x0, blocking collectives: 58.2 us -> none  [gather_in_order(): pieces = lax.all_gather(pieces, axes[k], axis=0, tiled=True)]
    all_gather x3, waiting for transfers between devices: 161 us -> 121 us  [total_of_pieces(): return lax.all_gather(value, axis).sum(0)]
    all_to_all x0 -> x3, blocking collectives: none -> 26.3 us  [gather_in_order(): tiles = lax.all_to_all(tiles, axes[k], split_axis=0, concat_axis=0)]
    all_to_all x0 -> x2, starting transfers between devices: none -> 11.8 us  [gather_in_order(): tiles = lax.all_to_all(tiles, axes[k], split_axis=0, concat_axis=0)]
    unnamed x13 -> x21, local copies, waits for them, and re-layouts: 67.8 us -> 68.5 us
  transfers between devices with their start and end apart: 6 -> 8, of which waited for: 3 -> 3; matrix products, arithmetic and copies ran while one was open for 27% -> 33% of each run, Pallas kernels for 0% -> 0%
where the time goes in v1:
time: 346 us; the launch traced here: 341 us
  waiting for transfers between devices  121 us (35%)
  local copies, waits for them, and re-layouts  112 us (32%)
  other arithmetic  37.3 us (11%)
  starting transfers between devices  30.1 us (9%)
  blocking collectives  26.3 us (8%)
  between operations  13.9 us (4%)
    all_gather x3, waiting for transfers between devices, total_of_pieces(): return lax.all_gather(value, axis).sum(0)  121 us
    unnamed x21, local copies, waits for them, and re-layouts  68.5 us
    all_to_all x3, blocking collectives, gather_in_order(): tiles = lax.all_to_all(tiles, axes[k], split_axis=0, concat_axis=0)  26.3 us
    unnamed x4, other arithmetic  20.6 us
    all_to_all x2, local copies, waits for them, and re-layouts, on_device(): lax.all_to_all(narrow_gate, SHARD, split_axis=2, concat_axis=1, tiled=True)  13.6 us
    all_to_all x2, local copies, waits for them, and re-layouts, on_device(): lax.all_to_all(narrow_up, SHARD, split_axis=2, concat_axis=1, tiled=True)  13.6 us
    all_to_all x2, local copies, waits for them, and re-layouts, on_device(): lax.all_to_all(narrow_down, SHARD, split_axis=1, concat_axis=2, tiled=True)  13.6 us
    all_to_all x2, starting transfers between devices, gather_in_order(): tiles = lax.all_to_all(tiles, axes[k], split_axis=0, concat_axis=0)  11.8 us
  transfers between devices with their start and end apart: 8, of which 3 were waited for; matrix products, arithmetic and copies ran while one was open for 33% of the time, Pallas kernels for 0%

profile of v1, /device:TPU:1, one launch (start us, length us, event | category | flops | bytes accessed | tf_op | source)
XLA Modules:
  0.0 340.7 jit_solution(9779688366531599395)
XLA Ops:
  7.2 3.4 %multiply_reduce_fusion.2 = f32[16,1024]{1,0:T(8,128)} fusion(f32[16,64,1024]{2,1,0:T(8,128)} %param.5), kind=kLoop, calls=%fused_computation.5 | loop fusion | flops 2080768 | bytes 4259840 | tf_op jit(solution)/shard_map/reduce_sum | solution.py:40
  10.7 3.4 %multiply_reduce_fusion.1 = f32[16,1024]{1,0:T(8,128)} fusion(f32[16,64,1024]{2,1,0:T(8,128)} %param.6), kind=kLoop, calls=%fused_computation.4 | loop fusion | flops 2080768 | bytes 4259840 | tf_op jit(solution)/shard_map/reduce_sum | solution.py:41
  14.3 8.8 %all_to_all.79 = bf16[2,2,512]{2,1,0:T(2,128)(2,1)S(1)} all-to-all(bf16[2,2,512]{2,1,0:T(2,128)(2,1)S(1)} %reshape.45), channel_id=1, replica_groups=mesh['expert_0'=2,'expert_1'=2,'shard_0'=4,'shard_1'=4,'shard_2'=2] {'sh..., dimensions={0} | all-to-all | bytes 8192 | tf_op jit(solution)/shard_map/all_to_all | solution.py:26
  23.3 9.0 %all_to_all.80 = bf16[4,2,1024]{2,1,0:T(2,128)(2,1)S(1)} all-to-all(bf16[4,2,1024]{2,1,0:T(2,128)(2,1)S(1)} %reshape.47), channel_id=1, replica_groups=mesh['expert_0'=2,'expert_1'=2,'shard_0'=4,'shard_1'=4,'shard_2'=2] {'sh..., dimensions={0} | all-to-all | bytes 32768 | tf_op jit(solution)/shard_map/all_to_all | solution.py:26
  32.6 8.5 %all_to_all.81 = bf16[4,2,4096]{2,1,0:T(2,128)(2,1)S(1)} all-to-all(bf16[4,2,4096]{2,1,0:T(2,128)(2,1)S(1)} %reshape.49), channel_id=1, replica_groups=mesh['expert_0'=2,'expert_1'=2,'shard_0'=4,'shard_1'=4,'shard_2'=2] {'sh..., dimensions={0} | all-to-all | bytes 131072 | tf_op jit(solution)/shard_map/all_to_all | solution.py:26
  42.2 3.4 all-to-all-start.6
  45.6 3.4 %multiply_reduce_fusion = f32[16,1024]{1,0:T(8,128)} fusion(f32[16,1024,64]{1,2,0:T(8,128)} %param.7), kind=kLoop, calls=%fused_computation.3 | loop fusion | flops 2080768 | bytes 4259840 | tf_op jit(solution)/shard_map/reduce_sum | solution.py:42
  49.0 8.1 %copy.49 = f32[16,64,1024]{1,0,2:T(8,128)} copy(f32[16,64,1024]{2,1,0:T(8,128)} %param.5) | data formatting | bytes 8388608 | tf_op args[0]
  57.9 8.5 %all-to-all-start.7 = ((bf16[2,2,2048,16]{2,3,1,0:T(8,128)(2,1)}), bf16[2,2,2048,16]{2,3,1,0:T(8,128)(2,1)S(1)}, u32[]{:S(2)}, u32[]{:S(2)}) async-start(bf16[2,2,2048,16]{2,3,1,0:T(8,128)(2,1)} %pad_maximum_fusion), calls=%async_computation.7 | async-start | bytes 524288 | tf_op jit(solution)/shard_map/all_to_all | solution.py:26
  66.4 16.8 %all-gather.7.cloned.1.call-done = f32[512,1024]{1,0:T(8,128)} async-done(((f32[16,1024]{1,0:T(8,128)}), f32[512,1024]{1,0:T(8,128)}) %all-gather.7.cloned.1.call-update) | async-done | bytes 2097168 | tf_op jit(solution)/shard_map/all_gather | solution.py:12
  85.1 6.9 %fusion.1 = bf16[1024,16,64]{2,1,0:T(8,128)(2,1)} fusion(f32[16,64,1024]{1,0,2:T(8,128)} %copy.49, f32[16,1024]{0,1:T(8,128)S(1)} %copy.48), kind=kLoop, calls=%fused_computation.14 | loop fusion | flops 2097152 | bytes 6356992
  91.9 7.9 %reshape.39 = bf16[32,2,16384]{2,1,0:T(2,128)(2,1)} reshape(bf16[1024,16,64]{2,1,0:T(8,128)(2,1)} %fusion.1) | data formatting | bytes 4194304
  99.8 5.9 %all-to-all-start = ((bf16[32,2,16384]{2,1,0:T(2,128)(2,1)}), bf16[32,2,16384]{2,1,0:T(2,128)(2,1)S(1)}, u32[]{:S(2)}, u32[]{:S(2)}) async-start(bf16[32,2,16384]{2,1,0:T(2,128)(2,1)} %reshape.39), calls=%async_computation | async-start | bytes 4194304 | tf_op jit(solution)/shard_map/all_to_all | solution.py:53
  105.7 8.1 %copy.53 = f32[16,64,1024]{1,0,2:T(8,128)} copy(f32[16,64,1024]{2,1,0:T(8,128)} %param.6) | data formatting | bytes 8388608 | tf_op args[1]
  113.8 51.8 %all-gather.9.cloned.1.call-done = f32[512,1024]{1,0:T(8,128)} async-done(((f32[16,1024]{1,0:T(8,128)}), f32[512,1024]{1,0:T(8,128)}) %all-gather.9.cloned.1.call-update) | async-done | bytes 2097168 | tf_op jit(solution)/shard_map/all_gather | solution.py:12
  167.5 6.9 %fusion.2 = bf16[1024,16,64]{2,1,0:T(8,128)(2,1)} fusion(f32[16,64,1024]{1,0,2:T(8,128)} %copy.53, f32[16,1024]{0,1:T(8,128)S(1)} %copy.52), kind=kLoop, calls=%fused_computation.15 | loop fusion | flops 2097152 | bytes 6356992
  174.4 7.9 %reshape.41 = bf16[32,2,16384]{2,1,0:T(2,128)(2,1)} reshape(bf16[1024,16,64]{2,1,0:T(8,128)(2,1)} %fusion.2) | data formatting | bytes 4194304
  182.3 6.2 %all-to-all-start.1 = ((bf16[32,2,16384]{2,1,0:T(2,128)(2,1)}), bf16[32,2,16384]{2,1,0:T(2,128)(2,1)}, u32[]{:S(2)}, u32[]{:S(2)}) async-start(bf16[32,2,16384]{2,1,0:T(2,128)(2,1)} %reshape.41), calls=%async_computation.1 | async-start | bytes 4194304 | tf_op jit(solution)/shard_map/all_to_all | solution.py:54
  188.5 8.1 %copy.57 = f32[16,1024,64]{2,0,1:T(8,128)} copy(f32[16,1024,64]{1,2,0:T(8,128)} %param.7) | data formatting | bytes 8388608 | tf_op args[2]
  196.6 52.2 %all-gather.11.cloned.1.call-done = f32[512,1024]{1,0:T(8,128)} async-done(((f32[16,1024]{1,0:T(8,128)}), f32[512,1024]{1,0:T(8,128)}) %all-gather.11.cloned.1.call-update) | async-done | bytes 2097168 | tf_op jit(solution)/shard_map/all_gather | solution.py:12
  250.7 6.9 %fusion.3 = bf16[1024,16,64]{2,1,0:T(8,128)(2,1)} fusion(f32[16,1024,64]{2,0,1:T(8,128)} %copy.57, f32[16,1024]{0,1:T(8,128)S(1)} %copy.56), kind=kLoop, calls=%fused_computation.16 | loop fusion | flops 2097152 | bytes 6356992
  257.5 7.9 %reshape.43 = bf16[32,2,16384]{2,1,0:T(2,128)(2,1)} reshape(bf16[1024,16,64]{2,1,0:T(8,128)(2,1)} %fusion.3) | data formatting | bytes 4194304
  265.4 6.0 %all-to-all-start.2 = ((bf16[32,2,16384]{2,1,0:T(2,128)(2,1)}), bf16[32,2,16384]{2,1,0:T(2,128)(2,1)}, u32[]{:S(2)}, u32[]{:S(2)}) async-start(bf16[32,2,16384]{2,1,0:T(2,128)(2,1)} %reshape.43), calls=%async_computation.2 | async-start | bytes 4194304 | tf_op jit(solution)/shard_map/all_to_all | solution.py:56
  273.5 4.0 %reshape.40 = bf16[1024,16,64]{2,1,0:T(8,128)(2,1)} reshape(bf16[32,2,16384]{2,1,0:T(2,128)(2,1)S(1)} %all-to-all-done) | data formatting | bytes 4194304
  277.5 6.9 %copy.51 = bf16[16,32,64,32]{2,1,3,0:T(8,128)(2,1)} copy(bf16[16,32,64,32]{2,0,3,1:T(8,128)(2,1)} %bitcast.58) | data formatting | bytes 4194304 | tf_op jit(solution)/shard_map/all_to_all | solution.py:53
  284.3 6.7 %all_to_all.57 = bf16[16,2048,32]{1,2,0:T(8,128)(2,1)} reshape(bf16[16,32,64,32]{2,1,3,0:T(8,128)(2,1)} %copy.51) | data formatting | bytes 4194304 | tf_op jit(solution)/shard_map/all_to_all | solution.py:53
  291.1 7.9 %reshape.42 = bf16[1024,16,64]{2,1,0:T(8,128)(2,1)} reshape(bf16[32,2,16384]{2,1,0:T(2,128)(2,1)} %all-to-all-done.1) | data formatting | bytes 4194304
  299.0 6.9 %copy.55 = bf16[16,32,64,32]{2,1,3,0:T(8,128)(2,1)} copy(bf16[16,32,64,32]{2,0,3,1:T(8,128)(2,1)} %bitcast.59) | data formatting | bytes 4194304 | tf_op jit(solution)/shard_map/all_to_all | solution.py:54
  305.9 6.7 %all_to_all.61 = bf16[16,2048,32]{1,2,0:T(8,128)(2,1)} reshape(bf16[16,32,64,32]{2,1,3,0:T(8,128)(2,1)} %copy.55) | data formatting | bytes 4194304 | tf_op jit(solution)/shard_map/all_to_all | solution.py:54
  312.6 7.9 %reshape.44 = bf16[1024,16,64]{2,1,0:T(8,128)(2,1)} reshape(bf16[32,2,16384]{2,1,0:T(2,128)(2,1)} %all-to-all-done.2) | data formatting | bytes 4194304
  320.6 6.9 %copy.59 = bf16[16,32,32,64]{3,2,1,0:T(8,128)(2,1)} copy(bf16[16,32,32,64]{3,0,1,2:T(8,128)(2,1)} %bitcast.60) | data formatting | bytes 4194304 | tf_op jit(solution)/shard_map/all_to_all | solution.py:56
  327.4 6.7 %all_to_all.65 = bf16[16,32,2048]{2,1,0:T(8,128)(2,1)} reshape(bf16[16,32,32,64]{3,2,1,0:T(8,128)(2,1)} %copy.59) | data formatting | bytes 4194304 | tf_op jit(solution)/shard_map/all_to_all | solution.py:56
  (42 shorter events, 10.4 us)
Async XLA Ops:
  7.2 7.0 %copy-start = (f32[64,16]{0,1:T(8,128)S(1)}, f32[64,16]{0,1:T(8,128)}, u32[]{:S(2)}) copy-start(f32[64,16]{0,1:T(8,128)} %param.8) | copy-start | bytes 12292
  7.2 7.0 %copy-start.1 = (f32[64]{0:T(128)S(1)}, f32[64]{0:T(128)}, u32[]{:S(2)}) copy-start(f32[64]{0:T(128)} %param.9) | copy-start | bytes 772
  7.2 76.0 %all-gather.7.cloned.1.call-start = ((), (), s32[]{:S(2)}) async-start(), calls=%async_computation.8 | async-start | bytes 2162688 | tf_op jit(solution)/shard_map/all_gather | solution.py:12
  10.7 154.9 %all-gather.9.cloned.1.call-start = ((), (), s32[]{:S(2)}) async-start(), calls=%async_computation.9 | async-start | bytes 2162688 | tf_op jit(solution)/shard_map/all_gather | solution.py:12
  42.2 15.0 %all-to-all-start.6 = ((bf16[2,1,2048,16]{2,3,1,0:T(8,128)(2,1)}), bf16[2,1,2048,16]{2,3,1,0:T(8,128)(2,1)S(1)}, u32[]{:S(2)}, u32[]{:S(2)}) async-start(bf16[2,1,2048,16]{2,3,1,0:T(8,128)(2,1)} %pad_maximum_fusion.1), calls=%async_computation.6 | async-start | bytes 262144 | tf_op jit(solution)/shard_map/all_to_all | solution.py:26
  45.5 203.2 %all-gather.11.cloned.1.call-start = ((), (), s32[]{:S(2)}) async-start(), calls=%async_computation.10 | async-start | bytes 2162688 | tf_op jit(solution)/shard_map/all_gather | solution.py:12
  57.9 41.9 %all-to-all-start.7 = ((bf16[2,2,2048,16]{2,3,1,0:T(8,128)(2,1)}), bf16[2,2,2048,16]{2,3,1,0:T(8,128)(2,1)S(1)}, u32[]{:S(2)}, u32[]{:S(2)}) async-start(bf16[2,2,2048,16]{2,3,1,0:T(8,128)(2,1)} %pad_maximum_fusion), calls=%async_computation.7 | async-start | bytes 524288 | tf_op jit(solution)/shard_map/all_to_all | solution.py:26
  99.8 82.4 %all-to-all-start = ((bf16[32,2,16384]{2,1,0:T(2,128)(2,1)}), bf16[32,2,16384]{2,1,0:T(2,128)(2,1)S(1)}, u32[]{:S(2)}, u32[]{:S(2)}) async-start(bf16[32,2,16384]{2,1,0:T(2,128)(2,1)} %reshape.39), calls=%async_computation | async-start | bytes 4194304 | tf_op jit(solution)/shard_map/all_to_all | solution.py:53
  182.3 83.1 %all-to-all-start.1 = ((bf16[32,2,16384]{2,1,0:T(2,128)(2,1)}), bf16[32,2,16384]{2,1,0:T(2,128)(2,1)}, u32[]{:S(2)}, u32[]{:S(2)}) async-start(bf16[32,2,16384]{2,1,0:T(2,128)(2,1)} %reshape.41), calls=%async_computation.1 | async-start | bytes 4194304 | tf_op jit(solution)/shard_map/all_to_all | solution.py:54
  265.4 47.2 %all-to-all-start.2 = ((bf16[32,2,16384]{2,1,0:T(2,128)(2,1)}), bf16[32,2,16384]{2,1,0:T(2,128)(2,1)}, u32[]{:S(2)}, u32[]{:S(2)}) async-start(bf16[32,2,16384]{2,1,0:T(2,128)(2,1)} %reshape.43), calls=%async_computation.2 | async-start | bytes 4194304 | tf_op jit(solution)/shard_map/all_to_all | solution.py:56
Sparse Core Ops, SparseCore 0:
  11.6 71.4 all-gather.6
  86.8 78.7 all-gather.8
  169.2 79.4 all-gather.10
